TPU v7x, 8 devices: a whole 2x2x1 slice. The times are simulated.
8 devices in a mesh: dp: 2 (over z, y), x: 4 (over x, core).
Axes of the slice: x: 2, y: 2, z: 1, core: 2. Of those that a mesh axis runs over, the one named last changes fastest.
Arguments:
- start_pos: int32 [256], P('dp'), parts along dimension 0
- hidden_in: bfloat16 [4, 256, 5120], P(None, ('dp', 'x')), parts along dimension 1
- k_cache: bfloat16 [256, 256, 8, 128], P('dp', None, 'x'), parts along dimension 0
- v_cache: bfloat16 [256, 256, 8, 128], P('dp', None, 'x'), parts along dimension 0
- attn_norm: bfloat16 [5120], replicated
- w_q: bfloat16 [5120, 8192], replicated
- w_k: bfloat16 [5120, 1024], replicated
- w_v: bfloat16 [5120, 1024], replicated
- q_norm: bfloat16 [128], replicated
- k_norm: bfloat16 [128], replicated
- w_o: bfloat16 [8192, 5120], replicated
- mlp_norm: bfloat16 [5120], replicated
- w_gate: bfloat16 [5120, 25600], replicated
- w_up: bfloat16 [5120, 25600], replicated
- w_down: bfloat16 [25600, 5120], replicated
Outputs:
- output 1: bfloat16 [4, 256, 5120], P(None, ('dp', 'x')), parts along dimension 1
- output 2: bfloat16 [256, 256, 8, 128], P(('dp', 'x')), parts along dimension 0
- output 3: bfloat16 [256, 256, 8, 128], P(('dp', 'x')), parts along dimension 0
There are 2 independent parts. A program takes and returns all parts, laid end to end along the dimension named above; an argument that names none is the same for every part.
All inputs are finite; a program needn't handle non-finite values.
Results may differ from a plain program's by a relative error of at most 0.0104383.
Values are sent between devices in bfloat16 or wider.
A program may use at most 4 GiB of HBM per device.

v0:
```python
import jax
import jax.numpy as jnp
from jax import lax
from jax.sharding import PartitionSpec as P

EPS = 1e-6
THETA = 1000000.0


def rms_norm(values, gain_vec):
    values32 = values.astype(jnp.float32)
    inv_rms = lax.rsqrt(jnp.mean(values32 * values32, axis=-1, keepdims=True) + EPS)
    return values32 * inv_rms * gain_vec.astype(jnp.float32)


def rotary(values, positions):
    head_dim = values.shape[-1]
    half_dim = head_dim // 2
    inv_freq = jnp.power(THETA, -jnp.arange(half_dim, dtype=jnp.float32) * 2.0 / head_dim)
    angles = positions.astype(jnp.float32)[..., None, None] * inv_freq
    cos_part = jnp.cos(angles)
    sin_part = jnp.sin(angles)
    first_half = values[..., :half_dim]
    second_half = values[..., half_dim:]
    return jnp.concatenate([first_half * cos_part - second_half * sin_part, second_half * cos_part + first_half * sin_part], axis=-1)


def project(hidden, positions, attn_norm, w_q, w_k, w_v, q_norm, k_norm):
    n_steps, num_rows = hidden.shape[0], hidden.shape[1]
    head_dim = q_norm.shape[0]
    normed = rms_norm(hidden, attn_norm).astype(jnp.bfloat16)
    queries = jnp.einsum('sbd,de->sbe', normed, w_q, preferred_element_type=jnp.float32).reshape(n_steps, num_rows, -1, head_dim)
    keys_new = jnp.einsum('sbd,de->sbe', normed, w_k, preferred_element_type=jnp.float32).reshape(n_steps, num_rows, -1, head_dim)
    values_new = jnp.einsum('sbd,de->sbe', normed, w_v, preferred_element_type=jnp.float32).reshape(n_steps, num_rows, -1, head_dim)
    queries = rotary(rms_norm(queries, q_norm), positions).astype(jnp.bfloat16)
    keys_new = rotary(rms_norm(keys_new, k_norm), positions).astype(jnp.bfloat16)
    return queries, keys_new, values_new.astype(jnp.bfloat16)


def attend(queries, cache_k, cache_v, keys_new, values_new, start_pos):
    n_steps, num_rows, n_heads, head_dim = queries.shape
    num_slots, kv_local = cache_k.shape[1], cache_k.shape[2]
    grouped = queries.reshape(n_steps, num_rows, kv_local, n_heads // kv_local, head_dim)
    score_scale = head_dim ** -0.5
    old_scores = jnp.einsum('sbkgd,btkd->bkgst', grouped, cache_k, preferred_element_type=jnp.float32) * score_scale
    old_valid = (jnp.arange(num_slots)[None, :] < start_pos[:, None])[:, None, None, None, :]
    old_scores = jnp.where(old_valid, old_scores, -jnp.inf)
    new_scores = jnp.einsum('sbkgd,jbkd->bkgsj', grouped, keys_new, preferred_element_type=jnp.float32) * score_scale
    new_valid = jnp.arange(n_steps)[:, None] >= jnp.arange(n_steps)[None, :]
    new_scores = jnp.where(new_valid, new_scores, -jnp.inf)
    peak_score = jnp.maximum(jnp.max(old_scores, axis=-1, keepdims=True), jnp.max(new_scores, axis=-1, keepdims=True))
    old_weights = jnp.exp(old_scores - peak_score)
    new_weights = jnp.exp(new_scores - peak_score)
    weight_sum = jnp.sum(old_weights, axis=-1) + jnp.sum(new_weights, axis=-1)
    mixed_vals = jnp.einsum('bkgst,btkd->sbkgd', old_weights.astype(jnp.bfloat16), cache_v, preferred_element_type=jnp.float32)
    mixed_vals = mixed_vals + jnp.einsum('bkgsj,jbkd->sbkgd', new_weights.astype(jnp.bfloat16), values_new, preferred_element_type=jnp.float32)
    mixed_vals = mixed_vals / jnp.transpose(weight_sum, (3, 0, 1, 2))[..., None]
    return mixed_vals.astype(jnp.bfloat16).reshape(n_steps, num_rows, n_heads, head_dim)


def finish(hidden, attended, w_o, mlp_norm, w_gate, w_up, w_down):
    n_steps, num_rows = attended.shape[0], attended.shape[1]
    flat_attn = attended.reshape(n_steps, num_rows, -1)
    attn_out = jnp.einsum('sbe,ed->sbd', flat_attn, w_o, preferred_element_type=jnp.float32)
    residual = (hidden.astype(jnp.float32) + attn_out).astype(jnp.bfloat16)
    normed = rms_norm(residual, mlp_norm).astype(jnp.bfloat16)
    gate_val = jnp.einsum('sbd,df->sbf', normed, w_gate, preferred_element_type=jnp.float32)
    up_val = jnp.einsum('sbd,df->sbf', normed, w_up, preferred_element_type=jnp.float32)
    activated = (jax.nn.silu(gate_val) * up_val).astype(jnp.bfloat16)
    down_val = jnp.einsum('sbf,fd->sbd', activated, w_down, preferred_element_type=jnp.float32)
    return (residual.astype(jnp.float32) + down_val).astype(jnp.bfloat16)


def write_slots(cache_arr, fresh_rows, start_pos):
    slot_ids = jnp.arange(cache_arr.shape[1])[None, :, None, None]
    for step_idx in range(fresh_rows.shape[0]):
        slot_hit = slot_ids == (start_pos + step_idx)[:, None, None, None]
        cache_arr = jnp.where(slot_hit, fresh_rows[step_idx][:, None], cache_arr)
    return cache_arr


def solution(mesh):
    row_spec = P(None, ('dp', 'x'), None)
    cache_in = P('dp', None, 'x', None)
    cache_out = P(('dp', 'x'), None, None, None)

    def local_run(start_pos, hidden_in, k_heads, v_heads, attn_norm, w_q, w_k, w_v, q_norm, k_norm, w_o, mlp_norm, w_gate, w_up, w_down):
        num_rows = hidden_in.shape[1]
        my_pos = lax.dynamic_slice_in_dim(start_pos, lax.axis_index('x') * num_rows, num_rows)
        k_local = lax.all_to_all(k_heads, 'x', 0, 2, tiled=True)
        v_local = lax.all_to_all(v_heads, 'x', 0, 2, tiled=True)
        positions = my_pos[None, :] + jnp.arange(hidden_in.shape[0])[:, None]
        queries, keys_new, values_new = project(hidden_in, positions, attn_norm, w_q, w_k, w_v, q_norm, k_norm)
        attended = attend(queries, k_local, v_local, keys_new, values_new, my_pos)
        out_hidden = finish(hidden_in, attended, w_o, mlp_norm, w_gate, w_up, w_down)
        return out_hidden, write_slots(k_local, keys_new, my_pos), write_slots(v_local, values_new, my_pos)

    return jax.shard_map(local_run, mesh=mesh, in_specs=(P('dp'), row_spec, cache_in, cache_in) + (P(),) * 11, out_specs=(row_spec, cache_out, cache_out), check_vma=False)
```

profile of v0, /device:TPU:0, one launch (start us, length us, event | category | flops | bytes accessed | tf_op | source)
XLA Modules:
  0.0 774.8 jit_solution(13824389113461511456)
XLA Ops:
  0.6 194.8 %all_to_all.36 = bf16[128,256,2,128]{3,2,1,0:T(2,128)(2,1)} all-to-all(bf16[128,256,2,128]{3,2,1,0:T(2,128)(2,1)} %param.17), channel_id=1, replica_groups=mesh['dp'=2,'x'=4] {'x'}, dimensions={0} | all-to-all | bytes 33554432 | tf_op jit(solution)/shard_map/all_to_all | solution.py:90
  195.5 0.0 copy-start.7
  195.5 0.0 copy-start.3
  195.5 7.1 all-to-all-start.1
  202.6 0.0 copy-done.8
  202.7 0.0 copy-done.9
  202.7 0.0 copy-done.5
  202.7 0.0 copy-done.6
  202.7 0.6 convert_element_type.74
  203.3 0.0 copy-done.7
  203.3 0.1 broadcast_add_fusion.2
  203.4 0.1 add_convert_fusion.2
  203.5 0.5 multiply_cosine_fusion
  204.1 0.0 copy-done.3
  204.1 0.4 fusion.60
  204.4 5.6 fusion.79
  210.1 5.5 fusion.25
  215.7 0.1 copy.74
  215.8 0.2 multiply_reduce_fusion.1
  216.0 0.1 copy.54
  216.1 0.1 copy.55
  216.3 30.5 %fusion.8 = f32[4,32,8192]{2,1,0:T(8,128)} fusion(bf16[5120,8192]{1,0:T(8,128)(2,1)} %param.20, bf16[4,32,5120]{2,1,0:T(8,128)(2,1)S(1)} %copy-done.3, f32[5120]{0:T(1024)S(1)} %convert_element_type.62, f32[4,32]{1,0:T(4,128)S(1)} %add_rsqrt_fusion.3), kind=kOutput, calls=%fused_computation.8 | convolution fusion | flops 10740039680 | bytes 89412096 | tf_op jit(solution)/shard_map/sbd,de->sbe/dot_general | solution.py:32
  246.8 2.9 copy.73
  249.7 0.4 fusion.87
  250.2 0.5 subtract_convert_fusion.1
  250.7 1.2 slice_maximum_fusion.3
  251.9 0.1 iota_compare_fusion.3
  252.0 0.1 iota_compare_fusion
  252.1 0.1 iota_compare_fusion.1
  252.2 0.0 slice-start
  252.2 1.2 fusion.52
  253.4 0.0 slice-start.1
  253.4 1.8 fusion.53
  255.2 0.0 slice-start.2
  255.2 0.0 slice-start.3
  255.2 3.1 fusion.63
  258.4 12.9 %fusion.95 = (f32[32,8,8,4]{2,3,1,0:T(4,128)S(1)}, f32[32,8,8,4,4]{2,4,3,1,0:T(4,128)}) fusion(bf16[4,32,8,64]{3,0,2,1:T(4,128)(2,1)S(1)} %get-tuple-element.20, bf16[4,32,8,64]{3,0,2,1:T(4,128)(2,1)S(1)} %get-tuple-element.19, pred[4,4]{1,0:T(4,128)(4,1)S(1)} %iota_compare_fusion.5, bf16[4,32,8,8,64]{4,3,2,1,0:T(8,128)(2,1)} %get-tuple-element.18, ...), kind=kOutput, calls=%fused_computation.117 | convolution fusion | flops 13197312 | bytes 2523152 | tf_op jit(solution)/shard_map/sbkgd,jbkd->bkgsj/dot_general | solution.py:48
  271.2 0.0 slice-done
  271.3 0.0 slice-done.1
  271.3 0.0 slice-done.2
  271.3 0.0 slice-done.3
  271.3 8.0 %copy.53 = bf16[4,32,256,2,128]{4,2,3,0,1:T(8,128)(2,1)} copy(bf16[4,32,256,2,128]{4,3,2,1,0:T(2,128)(2,1)S(1)} %bitcast.161) | data formatting | bytes 33554432 | tf_op jit(solution)/shard_map/all_to_all | solution.py:90
  279.3 106.1 %all-to-all-done.1 = bf16[128,256,2,128]{3,2,1,0:T(2,128)(2,1)} async-done(((bf16[128,256,2,128]{3,2,1,0:T(2,128)(2,1)}), bf16[128,256,2,128]{3,2,1,0:T(2,128)(2,1)}, u32[]{:S(2)}, u32[]{:S(2)}) %all-to-all-start.1) | async-done | bytes 16777248 | tf_op jit(solution)/shard_map/all_to_all | solution.py:91
  385.3 15.2 %copy.57 = bf16[4,32,256,2,128]{4,2,3,0,1:T(8,128)(2,1)} copy(bf16[4,32,256,2,128]{4,3,2,1,0:T(2,128)(2,1)} %bitcast.13) | data formatting | bytes 33554432 | tf_op jit(solution)/shard_map/all_to_all | solution.py:91
  400.5 11.8 %bitcast_reduce_fusion = (f32[32,8,8,4]{2,3,1,0:T(4,128)S(1)}, f32[32,8,4,8,256]{4,3,2,1,0:T(8,128)}) fusion(pred[32,256]{1,0:T(8,128)(4,1)S(1)} %get-tuple-element.36, bf16[32,256,8,128,1]{3,1,4,2,0:T(8,128)(2,1)} %bitcast.155, bf16[4,32,8,8,64]{4,3,2,1,0:T(8,128)(2,1)} %get-tuple-element.18, bf16[4,32,8,8,64]{4,3,2,1,0:T(8,128)(2,1)S(1)} %get-tuple-element.17), kind=kOutput, calls=%fused_computation.24 | convolution fusion | flops 547348480 | bytes 27303936 | tf_op jit(solution)/shard_map/sbkgd,btkd->bkgst/dot_general | solution.py:45
  412.3 0.2 max.8
  412.5 3.6 fusion.71
  416.1 0.0 copy-start
  416.1 6.0 fusion.29
  422.1 0.0 copy-done
  422.1 0.0 copy-start.4
  422.1 7.9 %fusion.50 = f32[32,8,8,4,128]{4,2,3,1,0:T(8,128)S(1)} fusion(bf16[32,256,8,128,1]{3,1,4,2,0:T(8,128)(2,1)} %bitcast.157, f32[32,8,4,8,256]{4,3,2,1,0:T(8,128)S(1)} %copy-done, f32[32,8,8,4]{2,3,1,0:T(4,128)S(1)} %max.8, pred[32,256]{1,0:T(8,128)(4,1)S(1)} %get-tuple-element.36), kind=kOutput, calls=%fused_computation.35 | convolution fusion | flops 545259520 | bytes 29401088 | tf_op jit(solution)/shard_map/bkgst,btkd->sbkgd/dot_general | solution.py:55
  430.0 0.2 add_bitcast_fusion
  430.2 2.5 fusion.55
  432.7 0.6 copy.59
  433.3 2.3 reshape_reshape.3
  435.6 29.2 %multiply_reduce_fusion = (f32[4,32]{1,0:T(4,128)S(1)}, f32[4,32,5120]{2,1,0:T(8,128)S(1)}) fusion(bf16[4,32,8192]{2,1,0:T(8,128)(2,1)} %reshape_reshape.3, bf16[8192,5120]{1,0:T(8,128)(2,1)} %param.25, bf16[4,32,5120]{2,1,0:T(8,128)(2,1)} %param.16), kind=kOutput, calls=%fused_computation.55 | convolution fusion | flops 10741350400 | bytes 89915904 | tf_op jit(solution)/shard_map/sbe,ed->sbd/dot_general | solution.py:64
  464.8 22.9 %select_select_fusion = (bf16[32,256,8,128]{3,1,2,0:T(8,128)(2,1)}, bf16[32,256,8,128]{3,1,2,0:T(8,128)(2,1)}) fusion(bf16[32,256,8,128]{3,1,2,0:T(8,128)(2,1)} %bitcast.158, pred[32,256]{1,0:T(8,128)(4,1)S(1)} %get-tuple-element.35, pred[32,256]{1,0:T(8,128)(4,1)S(1)} %get-tuple-element.43, pred[32,256]{1,0:T(8,128)(4,1)S(1)} %get-tuple-element.44, ...), kind=kLoop, calls=%fused_computation.12 | loop fusion | flops 67108864 | bytes 67665920 | tf_op jit(solution)/shard_map/jit(_where)/select_n | solution.py:78
  487.8 20.0 %copy.61 = bf16[32,256,8,128]{3,2,1,0:T(8,128)(2,1)} copy(bf16[32,256,8,128]{3,1,2,0:T(8,128)(2,1)} %get-tuple-element.29) | data formatting | bytes 33554432
  507.8 0.0 copy-done.1
  507.8 12.1 %copy.60 = bf16[32,256,8,128]{3,2,1,0:T(8,128)(2,1)} copy(bf16[32,256,8,128]{3,1,2,0:T(8,128)(2,1)S(1)} %copy-done.1) | data formatting | bytes 33554432
  519.9 84.3 %fusion.4 = f32[4,32,25600]{2,1,0:T(8,128)} fusion(bf16[5120,25600]{1,0:T(8,128)(2,1)} %param.27, f32[4,32,5120]{2,1,0:T(8,128)S(1)} %get-tuple-element.42, f32[5120]{0:T(1024)S(1)} %copy-done.2, f32[4,32]{1,0:T(4,128)S(1)} %add_rsqrt_fusion.2), kind=kOutput, calls=%fused_computation.4 | convolution fusion | flops 33556398080 | bytes 277893632 | tf_op jit(solution)/shard_map/sbd,df->sbf/dot_general | solution.py:67
  604.2 86.5 %fusion.13.clone.8 = bf16[4,32,25600]{2,1,0:T(8,128)(2,1)} fusion(bf16[5120,25600]{1,0:T(8,128)(2,1)} %param.28, f32[4,32,25600]{2,1,0:T(8,128)} %fusion.4, f32[4,32,5120]{2,1,0:T(8,128)S(1)} %get-tuple-element.42, f32[5120]{0:T(1024)S(1)} %copy-done.2, f32[4,32]{1,0:T(4,128)S(1)} %add_rsqrt_fusion.2), kind=kOutput, calls=%fused_computation.11.clone.clone.clone.clone.clone.clone.clone.1 | convolution fusion | flops 33576058880 | bytes 284447232 | tf_op jit(solution)/shard_map/sbd,df->sbf/dot_general | solution.py:68
  690.7 83.7 %fusion.45 = bf16[4,32,5120]{2,1,0:T(8,128)(2,1)} fusion(f32[4,32,5120]{2,1,0:T(8,128)S(1)} %get-tuple-element.42, bf16[25600,5120]{1,0:T(8,128)(2,1)} %param.29, bf16[4,32,25600]{2,1,0:T(8,128)(2,1)} %fusion.13.clone.8), kind=kOutput, calls=%fused_computation.34 | convolution fusion | flops 33555742720 | bytes 272629760 | tf_op jit(solution)/shard_map/sbf,fd->sbd/dot_general | solution.py:70
  (30 shorter events, 0.3 us)
Async XLA Ops:
  195.5 7.2 copy-start.8
  195.5 7.2 copy-start.9
  195.5 7.2 copy-start.5
  195.5 7.2 copy-start.6
  195.5 7.9 %copy-start.7 = (s32[128]{0:T(128)S(1)}, s32[128]{0:T(128)}, u32[]{:S(2)}) copy-start(s32[128]{0:T(128)} %param.15) | copy-start | bytes 1540
  195.5 8.6 %copy-start.3 = (bf16[4,32,5120]{2,1,0:T(8,128)(2,1)S(1)}, bf16[4,32,5120]{2,1,0:T(8,128)(2,1)}, u32[]{:S(2)}) copy-start(bf16[4,32,5120]{2,1,0:T(8,128)(2,1)} %param.16) | copy-start | bytes 3932164
  195.5 189.8 %all-to-all-start.1 = ((bf16[128,256,2,128]{3,2,1,0:T(2,128)(2,1)}), bf16[128,256,2,128]{3,2,1,0:T(2,128)(2,1)}, u32[]{:S(2)}, u32[]{:S(2)}) async-start(bf16[128,256,2,128]{3,2,1,0:T(2,128)(2,1)} %param.18), calls=%async_computation.1 | async-start | bytes 33554432 | tf_op jit(solution)/shard_map/all_to_all | solution.py:91
  252.2 19.1 %slice-start = ((s8[16777216]{0:T(1024)(128)(4,1)}), s8[4194304]{0:T(1024)(128)(4,1)S(1)}, s32[]{:S(2)}) async-start(s8[16777216]{0:T(1024)(128)(4,1)} %bitcast.159), calls=%async_computation.2 | async-start | bytes 8388608
  253.4 17.8 %slice-start.1 = ((s8[16777216]{0:T(1024)(128)(4,1)}), s8[4194304]{0:T(1024)(128)(4,1)S(1)}, s32[]{:S(2)}) async-start(s8[16777216]{0:T(1024)(128)(4,1)} %bitcast.159), calls=%async_computation.3 | async-start | bytes 8388608
  255.2 16.1 %slice-start.2 = ((s8[16777216]{0:T(1024)(128)(4,1)}), s8[4194304]{0:T(1024)(128)(4,1)S(1)}, s32[]{:S(2)}) async-start(s8[16777216]{0:T(1024)(128)(4,1)} %bitcast.159), calls=%async_computation.4 | async-start | bytes 8388608
  255.2 16.1 %slice-start.3 = ((s8[16777216]{0:T(1024)(128)(4,1)}), s8[4194304]{0:T(1024)(128)(4,1)S(1)}, s32[]{:S(2)}) async-start(s8[16777216]{0:T(1024)(128)(4,1)} %bitcast.159), calls=%async_computation.5 | async-start | bytes 8388608
  416.1 6.0 copy-start
  422.1 8.1 %copy-start.4 = (f32[32,8,8,4,4]{2,4,3,1,0:T(4,128)S(1)}, f32[32,8,8,4,4]{2,4,3,1,0:T(4,128)}, u32[]{:S(2)}) copy-start(f32[32,8,8,4,4]{2,4,3,1,0:T(4,128)} %get-tuple-element.40) | copy-start | bytes 393220
  487.7 20.0 %copy-start.1 = (bf16[32,256,8,128]{3,1,2,0:T(8,128)(2,1)S(1)}, bf16[32,256,8,128]{3,1,2,0:T(8,128)(2,1)}, u32[]{:S(2)}) copy-start(bf16[32,256,8,128]{3,1,2,0:T(8,128)(2,1)} %get-tuple-element.30) | copy-start | bytes 50331652
  507.8 12.1 %copy-start.2 = (f32[5120]{0:T(1024)S(1)}, f32[5120]{0:T(1024)}, u32[]{:S(2)}) copy-start(f32[5120]{0:T(1024)} %convert_element_type.74) | copy-start | bytes 61444
where the time goes:
time: 784 us; the launch traced here: 775 us
  matrix products  360 us (46%)
  blocking collectives  195 us (25%)
  waiting for transfers between devices  106 us (14%)
  local copies, waits for them, and re-layouts  61.7 us (8%)
  other arithmetic  43.2 us (6%)
    all_to_all x1, blocking collectives, local_run(): k_local = lax.all_to_all(k_heads, 'x', 0, 2, tiled=True)  195 us
    all_to_all x1, waiting for transfers between devices, local_run(): v_local = lax.all_to_all(v_heads, 'x', 0, 2, tiled=True)  106 us
    dot_general x1, matrix products, finish(): jnp.einsum('sbd,df->sbf', normed, w_up, preferred_element_type=jnp.float32)  86.5 us
    dot_general x1, matrix products, finish(): jnp.einsum('sbd,df->sbf', normed, w_gate, preferred_element_type=jnp.floa...  84.3 us
    dot_general x1, matrix products, finish(): jnp.einsum('sbf,fd->sbd', activated, w_down, preferred_element_type=jnp.f...  83.7 us
    unnamed x40, local copies, waits for them, and re-layouts  35.4 us
    dot_general x1, matrix products, project(): jnp.einsum('sbd,de->sbe', normed, w_q, preferred_element_type=jnp.float32)  30.5 us
    dot_general x1, matrix products, finish(): jnp.einsum('sbe,ed->sbd', flat_attn, w_o, preferred_element_type=jnp.floa...  29.2 us
  transfers between devices with their start and end apart: 1, of which 1 were waited for; matrix products, arithmetic and copies ran while one was open for 10% of the time, Pallas kernels for 0%

commit v1 on v0

v1 whole, which is shorter than its diff:
```python
import jax
import jax.numpy as jnp
from jax import lax
from jax.experimental import pallas as pl
from jax.experimental.pallas import tpu as pltpu
from jax.sharding import PartitionSpec as P

EPS = 1e-6
THETA = 1000000.0
F32 = jnp.float32
BF16 = jnp.bfloat16
MESH = pl.DeviceIdType.MESH

STEPS = 4
ROWS = 32
TOK = STEPS * ROWS
GROUP = 128
D = 5120
HD = 128
QH = 16
FF = 25600
T = 256


def rms_norm(values, gain_vec):
    values32 = values.astype(F32)
    inv_rms = lax.rsqrt(jnp.mean(values32 * values32, axis=-1, keepdims=True) + EPS)
    return values32 * inv_rms * gain_vec.astype(F32)


def partners(me):
    c1 = me + 1 - 2 * lax.rem(me, 2)
    c2 = lax.rem(me + 2, 4)
    c3 = 3 - me
    return c1, c2, c3


def greet(devices):
    barrier = pltpu.get_barrier_semaphore()
    for dev in devices:
        pl.semaphore_signal(barrier, inc=1, device_id={"x": dev}, device_id_type=MESH)
    pl.semaphore_wait(barrier, len(devices))


def remote(src, dst, ssem, rsem, dev):
    return pltpu.make_async_remote_copy(
        src_ref=src, dst_ref=dst, send_sem=ssem, recv_sem=rsem,
        device_id={"x": dev}, device_id_type=MESH)


def qkv_kernel(hn, cos, sin, qg, kg, wq, wk, wv, q_out, kn_out, vn_out,
               hall, ws, qscr, kscr, vscr, wsem, s1, r1, s2, r2, sf, rf):
    me = lax.axis_index("x")
    c1, c2, c3 = partners(me)

    wcopies = []
    for c in range(10):
        if c < 8:
            src = wq.at[:, pl.ds(pl.multiple_of(me * 2048 + c * 256, 256), 256)]
        else:
            src = (wk if c == 8 else wv).at[:, pl.ds(pl.multiple_of(me * 256, 256), 256)]
        wcopies.append(pltpu.make_async_copy(src, ws.at[c], wsem.at[c]))

    greet((c1, c2))
    cross = []
    for s in range(STEPS):
        row = 256 + (s // 2) * 128 + (s % 2) * 32
        cp = remote(hn.at[pl.ds(s * 32, 32)], hall.at[pl.ds(row, 32)], s2.at[s], r2.at[s], c2)
        cp.start()
        cross.append(cp)
    near = remote(hn, hall.at[pl.ds(128, 128)], s1, r1, c1)
    near.start()
    for cp in wcopies:
        cp.start()
    hall[pl.ds(0, 128), :] = hn[...]

    fwd = []
    for s in range(STEPS):
        row = 256 + (s // 2) * 128 + (s % 2) * 32
        fwd.append(remote(hall.at[pl.ds(row, 32)], hall.at[pl.ds(row + 64, 32)], sf.at[s], rf.at[s], c1))

    def table(ref, groups):
        return jnp.concatenate([ref[j * STEPS + s] for j, s in groups], axis=0)

    for blk in range(4):
        if blk == 0:
            groups = [(me, s) for s in range(4)]
        elif blk == 1:
            near.wait_recv()
            groups = [(c1, s) for s in range(4)]
        else:
            lo = (blk - 2) * 2
            for s in (lo, lo + 1):
                cross[s].wait_recv()
                fwd[s].start()
            for s in (lo, lo + 1):
                fwd[s].wait_recv()
            groups = [(c2, lo), (c2, lo + 1), (c3, lo), (c3, lo + 1)]
        cos_b = table(cos, groups)
        sin_b = table(sin, groups)

        def head(val, gain, cos_b=cos_b, sin_b=sin_b):
            inv = lax.rsqrt(jnp.mean(val * val, axis=-1, keepdims=True) + EPS)
            val = val * inv * gain
            return val * cos_b + pltpu.roll(val, 64, 1) * sin_b

        def project(c, blk=blk):
            return jnp.dot(hall[pl.ds(blk * 128, 128), :], ws[c], preferred_element_type=F32)

        def q_chunk(c, carry, blk=blk, head=head, project=project):
            acc = project(c)
            for hh in range(2):
                qscr[pl.ds(2 * c + hh, 128, stride=QH), :] = head(acc[:, hh * HD:(hh + 1) * HD], qg[...])
            return carry

        if blk == 0:
            for c in range(8):
                wcopies[c].wait()
        lax.fori_loop(0, 8, q_chunk, 0)
        if blk == 0:
            wcopies[8].wait()
            wcopies[9].wait()
        k_acc = project(8)
        v_acc = project(9)
        for hh in range(2):
            k_head = head(k_acc[:, hh * HD:(hh + 1) * HD], kg[...])
            v_head = v_acc[:, hh * HD:(hh + 1) * HD]
            for g, (j, s) in enumerate(groups):
                at = pl.ds(j * 256 + s * 2 + hh, 32, stride=8)
                kscr[at, :] = k_head[g * 32:(g + 1) * 32]
                vscr[at, :] = v_head[g * 32:(g + 1) * 32]
        for g, (j, s) in enumerate(groups):
            q_out[s, pl.ds(j * 32, 32)] = qscr[pl.ds(g * 512, 512), :].reshape(32, QH, HD).astype(BF16)
    kn_out[...] = kscr[...].reshape(GROUP, 8, HD).astype(BF16)
    vn_out[...] = vscr[...].reshape(GROUP, 8, HD).astype(BF16)
    for s in range(STEPS):
        cross[s].wait_send()
        fwd[s].wait_send()
    near.wait_send()


def qkv(hn, cos, sin, qg, kg, wq, wk, wv):
    vmem = pl.BlockSpec(memory_space=pltpu.VMEM)
    hbm = pl.BlockSpec(memory_space=pl.ANY)
    dma = pltpu.SemaphoreType.DMA
    return pl.pallas_call(
        qkv_kernel,
        out_shape=(jax.ShapeDtypeStruct((STEPS, GROUP, QH, HD), BF16),
                   jax.ShapeDtypeStruct((GROUP, 8, HD), BF16),
                   jax.ShapeDtypeStruct((GROUP, 8, HD), BF16)),
        in_specs=[vmem] * 5 + [hbm] * 3,
        out_specs=(vmem,) * 3,
        scratch_shapes=[
            pltpu.VMEM((512, D), BF16), pltpu.VMEM((10, D, 256), BF16),
            pltpu.VMEM((128 * QH, HD), F32), pltpu.VMEM((GROUP * 8, HD), F32), pltpu.VMEM((GROUP * 8, HD), F32),
            dma((10,)), dma, dma, dma((4,)), dma((4,)), dma((4,)), dma((4,))],
        compiler_params=pltpu.CompilerParams(collective_id=0, has_side_effects=True, vmem_limit_bytes=60 << 20),
        cost_estimate=pl.CostEstimate(flops=2 * 512 * D * 2560, bytes_accessed=30 << 20, transcendentals=0),
        name="qkv",
    )(hn, cos, sin, qg, kg, wq, wk, wv)


SEQ = 4
PER = ROWS // SEQ


def attn_kernel(pos, q, kc, vc, kn, vn, kn_src, vn_src, o_rx, kn_rx, vn_rx,
                oscr, osend, so, ro, sk, rk, sv, rv, lsem):
    step = pl.program_id(0)
    me = lax.axis_index("x")
    c1, c2, c3 = partners(me)
    order = (c2, c3, c1, me)

    def o_copy(k):
        return remote(osend.at[k], o_rx.at[pl.ds(me * 4, 4)], so.at[k], ro.at[k], order[k])

    def n_copy(k, src, dst, ss, rs):
        return remote(src.at[pl.ds(order[k] * ROWS, ROWS)], dst.at[:, :, me], ss.at[k], rs.at[k], order[k])

    def own_copies():
        return (pltpu.make_async_copy(osend.at[3], o_rx.at[pl.ds(me * 4, 4)], lsem.at[0]),
                pltpu.make_async_copy(kn_src.at[pl.ds(me * ROWS, ROWS)], kn_rx.at[:, :, me], lsem.at[1]),
                pltpu.make_async_copy(vn_src.at[pl.ds(me * ROWS, ROWS)], vn_rx.at[:, :, me], lsem.at[2]))

    @pl.when(step == 0)
    def _():
        greet((c1, c2, c3))
        for k in range(3):
            n_copy(k, kn_src, kn_rx, sk, rk).start()
            n_copy(k, vn_src, vn_rx, sv, rv).start()
        own_copies()[1].start()
        own_copies()[2].start()

    for k in range(3):
        @pl.when(step == (k + 1) * PER)
        def _(k=k):
            o_copy(k).start()

    which = step // PER
    dest = jnp.where(which == 0, c2, jnp.where(which == 1, c3, jnp.where(which == 2, c1, me)))
    base = dest * ROWS + lax.rem(step, PER) * SEQ
    row = lax.broadcasted_iota(jnp.int32, (64, 2 * T), 0)
    col = lax.broadcasted_iota(jnp.int32, (64, 2 * T), 1)
    same_head = lax.rem(row // 8, 2) == lax.rem(col, 2)
    nrow = lax.broadcasted_iota(jnp.int32, (64, 8), 0)
    ncol = lax.broadcasted_iota(jnp.int32, (64, 8), 1)
    new_ok = (lax.rem(nrow // 8, 2) == lax.rem(ncol, 2)) & (ncol // 2 <= nrow // 16)
    scale = HD ** -0.5
    dims = (((1,), (1,)), ((), ()))
    for i in range(SEQ):
        start = pos[base + i]
        q2 = q[:, i].reshape(64, HD)
        s_old = lax.dot_general(q2, kc[i], dims, preferred_element_type=F32) * scale
        s_old = jnp.where(same_head & (col < 2 * start), s_old, -jnp.inf)
        s_new = lax.dot_general(q2, kn[i], dims, preferred_element_type=F32) * scale
        s_new = jnp.where(new_ok, s_new, -jnp.inf)
        peak = jnp.maximum(jnp.max(s_old, axis=-1, keepdims=True), jnp.max(s_new, axis=-1, keepdims=True))
        w_old = jnp.exp(s_old - peak)
        w_new = jnp.exp(s_new - peak)
        total = jnp.sum(w_old, axis=-1, keepdims=True) + jnp.sum(w_new, axis=-1, keepdims=True)
        mixed = jnp.dot(w_old.astype(BF16), vc[i], preferred_element_type=F32)
        mixed = mixed + jnp.dot(w_new.astype(BF16), vn[i], preferred_element_type=F32)
        oscr[pl.ds(lax.rem(step, PER) * SEQ + i, 64, stride=ROWS), :] = mixed / total

    @pl.when(lax.rem(step, PER) == PER - 1)
    def _():
        for s in range(STEPS):
            for hg in range(QH):
                osend[which, hg // 4, s * ROWS:(s + 1) * ROWS, (hg % 4) * HD:(hg % 4 + 1) * HD] = (
                    oscr[pl.ds((s * QH + hg) * ROWS, ROWS), :].astype(BF16))

    @pl.when(step == 4 * PER - 1)
    def _():
        own_copies()[0].start()
        for cp in own_copies():
            cp.wait()
        for k in range(3):
            o_copy(k).wait()
            n_copy(k, kn_src, kn_rx, sk, rk).wait()
            n_copy(k, vn_src, vn_rx, sv, rv).wait()


def attention(pos, q, kc, vc, kn, vn):
    hbm = pl.BlockSpec(memory_space=pl.ANY)
    dma = pltpu.SemaphoreType.DMA

    def block(step):
        me = lax.axis_index("x")
        c1, c2, c3 = partners(me)
        which = step // PER
        dest = jnp.where(which == 0, c2, jnp.where(which == 1, c3, jnp.where(which == 2, c1, me)))
        return dest * PER + lax.rem(step, PER)

    seq = lambda rows: pl.BlockSpec((SEQ, rows, HD), lambda i: (block(i), 0, 0))
    new = jax.ShapeDtypeStruct((ROWS, STEPS, 4, 2, HD), BF16)
    return pl.pallas_call(
        attn_kernel,
        grid=(4 * PER,),
        out_shape=(jax.ShapeDtypeStruct((16, TOK, 512), BF16), new, new),
        in_specs=[pl.BlockSpec(memory_space=pltpu.SMEM),
                  pl.BlockSpec((STEPS, SEQ, QH, HD), lambda i: (0, block(i), 0, 0)),
                  seq(2 * T), seq(2 * T), seq(8), seq(8), hbm, hbm],
        out_specs=(hbm,) * 3,
        scratch_shapes=[
            pltpu.VMEM((64 * ROWS, HD), F32), pltpu.VMEM((4, 4, TOK, 512), BF16),
            dma((3,)), dma((3,)), dma((3,)), dma((3,)), dma((3,)), dma((3,)), dma((3,))],
        compiler_params=pltpu.CompilerParams(collective_id=1, has_side_effects=True, vmem_limit_bytes=40 << 20),
        cost_estimate=pl.CostEstimate(flops=4 * 128 * 64 * 512 * 128, bytes_accessed=36 << 20, transcendentals=0),
        name="attention",
    )(pos, q, kc.reshape(GROUP, 2 * T, HD), vc.reshape(GROUP, 2 * T, HD), kn, vn,
      kn.reshape(GROUP, STEPS, 2, HD), vn.reshape(GROUP, STEPS, 2, HD))


NB = 3
N_O = 16
N_C = FF // 256
N_D = FF // 512


def mlp_kernel(o, hid, gain, wo, wg, wu, wd, kc, vc, out, k_rx, v_rx,
               wrow, wcol, acc, x1, z, g, rsem, csem, ks, kr, vs, vr):
    me = lax.axis_index("x")
    c1, c2, c3 = partners(me)
    order = (c2, c3, c1)

    def row_o(i):
        slot = lax.rem(i, NB)
        return pltpu.make_async_copy(wo.at[pl.ds(i * 512, 512)], wrow.at[slot], rsem.at[slot])

    def row_d(i):
        slot = lax.rem(i + N_O, NB)
        return pltpu.make_async_copy(wd.at[pl.ds(i * 512, 512)], wrow.at[slot], rsem.at[slot])

    def col(i):
        slot = lax.rem(i, NB)
        at = pl.ds(pl.multiple_of(i * 256, 256), 256)
        return (pltpu.make_async_copy(wg.at[:, at], wcol.at[slot, 0], csem.at[slot, 0]),
                pltpu.make_async_copy(wu.at[:, at], wcol.at[slot, 1], csem.at[slot, 1]))

    for i in range(NB):
        row_o(i).start()
    greet((c1, c2, c3))
    bulk = []
    for k in range(3):
        for src, dst, ss, rs in ((kc, k_rx, ks, kr), (vc, v_rx, vs, vr)):
            bulk.append(remote(src.at[pl.ds(order[k] * ROWS, ROWS)], dst.at[k], ss.at[k], rs.at[k], order[k]))
    for cp in bulk:
        cp.start()
    for i in range(NB):
        for cp in col(i):
            cp.start()

    def accumulate(lhs, slot, first):
        for n in range(10):
            cols = slice(n * 512, (n + 1) * 512)
            part = jnp.dot(lhs, wrow[slot, :, cols], preferred_element_type=F32)
            acc[:, cols] = acc[:, cols] + part

    acc[...] = jnp.zeros_like(acc)

    def o_step(i, carry):
        row_o(i).wait()
        accumulate(o[i], lax.rem(i, NB), i == 0)

        @pl.when(i + NB < N_O)
        def _():
            row_o(i + NB).start()

        @pl.when(i + NB >= N_O)
        def _():
            row_d(i + NB - N_O).start()
        return carry

    lax.fori_loop(0, N_O, o_step, 0)

    def norm_step(r, carry):
        rows = pl.ds(r * 16, 16)
        res = (hid[rows, :].astype(F32) + acc[rows, :]).astype(BF16)
        x1[rows, :] = res
        res = res.astype(F32)
        inv = lax.rsqrt(jnp.mean(res * res, axis=-1, keepdims=True) + EPS)
        z[rows, :] = (res * inv * gain[...]).astype(BF16)
        acc[rows, :] = jnp.zeros((16, D), F32)
        return carry

    lax.fori_loop(0, TOK // 16, norm_step, 0)

    def col_step(i, carry):
        slot = lax.rem(i, NB)
        for cp in col(i):
            cp.wait()
        gate = jnp.dot(z[...], wcol[slot, 0], preferred_element_type=F32)
        up = jnp.dot(z[...], wcol[slot, 1], preferred_element_type=F32)
        g[i // 2, :, pl.ds(pl.multiple_of(lax.rem(i, 2) * 256, 256), 256)] = (
            gate * jax.nn.sigmoid(gate) * up).astype(BF16)

        @pl.when(i + NB < N_C)
        def _():
            for cp in col(i + NB):
                cp.start()
        return carry

    lax.fori_loop(0, N_C, col_step, 0)

    def d_step(i, carry):
        row_d(i).wait()
        accumulate(g[i], lax.rem(i + N_O, NB), i == 0)

        @pl.when(i + NB < N_D)
        def _():
            row_d(i + NB).start()
        return carry

    lax.fori_loop(0, N_D, d_step, 0)

    def out_step(r, carry):
        rows = pl.ds(r * 16, 16)
        out[rows, :] = (x1[rows, :].astype(F32) + acc[rows, :]).astype(BF16)
        return carry

    lax.fori_loop(0, TOK // 16, out_step, 0)
    for cp in bulk:
        cp.wait()


def mlp(o, hid, gain, wo, wg, wu, wd, kc, vc):
    vmem = pl.BlockSpec(memory_space=pltpu.VMEM)
    hbm = pl.BlockSpec(memory_space=pl.ANY)
    dma = pltpu.SemaphoreType.DMA
    rx = jax.ShapeDtypeStruct((3, ROWS, T, 2, HD), BF16)
    return pl.pallas_call(
        mlp_kernel,
        out_shape=(jax.ShapeDtypeStruct((TOK, D), BF16), rx, rx),
        in_specs=[vmem] * 3 + [hbm] * 6,
        out_specs=(vmem, hbm, hbm),
        scratch_shapes=[
            pltpu.VMEM((NB, 512, D), BF16), pltpu.VMEM((NB, 2, D, 256), BF16),
            pltpu.VMEM((TOK, D), F32), pltpu.VMEM((TOK, D), BF16), pltpu.VMEM((TOK, D), BF16),
            pltpu.VMEM((N_D, TOK, 512), BF16),
            dma((NB,)), dma((NB, 2)), dma((3,)), dma((3,)), dma((3,)), dma((3,))],
        compiler_params=pltpu.CompilerParams(collective_id=2, has_side_effects=True, vmem_limit_bytes=60 << 20),
        cost_estimate=pl.CostEstimate(flops=2 * TOK * D * (8192 + 3 * FF), bytes_accessed=900 << 20, transcendentals=0),
        name="mlp",
    )(o, hid, gain, wo, wg, wu, wd, kc, vc)


AB = 2
AR = 4


def place_kernel(pos, kc, vc, k_rx, v_rx, kn, vn, k_out, v_out, kbuf, vbuf, isem, osem):
    me = lax.axis_index("x")
    c1, c2, c3 = partners(me)
    n_pieces = ROWS // AB
    arrays = ((kc, k_rx, kn, k_out, kbuf), (vc, v_rx, vn, v_out, vbuf))

    def loads(i):
        slot = lax.rem(i, AR)
        copies = []
        for a, (own, rx, _, _, buf) in enumerate(arrays):
            for k, dev in enumerate((c2, c3, c1)):
                copies.append(pltpu.make_async_copy(
                    rx.at[k, pl.ds(i * AB, AB)], buf.at[slot, :, :, dev], isem.at[slot, a, k]))
            copies.append(pltpu.make_async_copy(
                own.at[pl.ds(me * ROWS + i * AB, AB)], buf.at[slot, :, :, me], isem.at[slot, a, 3]))
        return copies

    def stores(i):
        slot = lax.rem(i, AR)
        return [pltpu.make_async_copy(buf.at[slot], out.at[pl.ds(i * AB, AB)], osem.at[slot, a])
                for a, (_, _, _, out, buf) in enumerate(arrays)]

    for i in range(AR - 1):
        for cp in loads(i):
            cp.start()

    def piece(i, carry):
        slot = lax.rem(i, AR)
        for cp in loads(i):
            cp.wait()
        for b in range(AB):
            start = pos[i * AB + b]
            for _, _, new, _, buf in arrays:
                for s in range(STEPS):
                    buf[slot, b, start + s] = new[i * AB + b, s]
        for cp in stores(i):
            cp.start()

        @pl.when(i >= 1)
        def _():
            for cp in stores(i - 1):
                cp.wait()

        @pl.when(i + AR - 1 < n_pieces)
        def _():
            for cp in loads(i + AR - 1):
                cp.start()
        return carry

    lax.fori_loop(0, n_pieces, piece, 0)
    for cp in stores(n_pieces - 1):
        cp.wait()


def place(pos, kc, vc, k_rx, v_rx, kn, vn):
    hbm = pl.BlockSpec(memory_space=pl.ANY)
    vmem = pl.BlockSpec(memory_space=pltpu.VMEM)
    out = jax.ShapeDtypeStruct((ROWS, T, 4, 2, HD), BF16)
    buf = pltpu.VMEM((AR, AB, T, 4, 2, HD), BF16)
    dma = pltpu.SemaphoreType.DMA
    return pl.pallas_call(
        place_kernel,
        out_shape=(out, out),
        in_specs=[pl.BlockSpec(memory_space=pltpu.SMEM)] + [hbm] * 4 + [vmem] * 2,
        out_specs=(hbm, hbm),
        scratch_shapes=[buf, buf, dma((AR, 2, 4)), dma((AR, 2))],
        compiler_params=pltpu.CompilerParams(vmem_limit_bytes=40 << 20),
        cost_estimate=pl.CostEstimate(flops=1 << 20, bytes_accessed=68 << 20, transcendentals=0),
        name="place",
    )(pos, kc, vc, k_rx, v_rx, kn, vn)


def solution(mesh):
    row_spec = P(None, ('dp', 'x'), None)
    cache_in = P('dp', None, 'x', None)
    cache_out = P(('dp', 'x'), None, None, None)

    def local_run(start_pos, hidden_in, k_heads, v_heads, attn_norm, w_q, w_k, w_v, q_norm, k_norm, w_o, mlp_norm, w_gate, w_up, w_down):
        my_pos = lax.dynamic_slice_in_dim(start_pos, lax.axis_index('x') * ROWS, ROWS)
        hid = hidden_in.reshape(TOK, D)
        hn = rms_norm(hid, attn_norm).astype(BF16)

        inv_freq = jnp.power(THETA, -jnp.arange(HD // 2, dtype=F32) * 2.0 / HD)
        positions = start_pos.reshape(4, 1, ROWS) + jnp.arange(STEPS)[None, :, None]
        angles = positions.astype(F32)[..., None] * inv_freq
        cos = jnp.cos(angles)
        sin = jnp.sin(angles)
        cos = jnp.concatenate([cos, cos], axis=-1).reshape(16, ROWS, HD)
        sin = jnp.concatenate([-sin, sin], axis=-1).reshape(16, ROWS, HD)

        q, kn, vn = qkv(hn, cos, sin, q_norm.astype(F32)[None], k_norm.astype(F32)[None], w_q, w_k, w_v)
        o, kn_rx, vn_rx = attention(start_pos, q, k_heads, v_heads, kn, vn)
        out, k_rx, v_rx = mlp(o, hid, mlp_norm.astype(F32)[None], w_o, w_gate, w_up, w_down, k_heads, v_heads)
        k_out, v_out = place(my_pos, k_heads, v_heads, k_rx, v_rx, kn_rx, vn_rx)
        return (out.reshape(STEPS, ROWS, D), k_out.reshape(ROWS, T, 8, HD), v_out.reshape(ROWS, T, 8, HD))

    return jax.shard_map(local_run, mesh=mesh, in_specs=(P('dp'), row_spec, cache_in, cache_in) + (P(),) * 11, out_specs=(row_spec, cache_out, cache_out), check_vma=False)
```

time: 784 us -> 501 us (0.64); the launches traced: 775 us -> 500 us
  Pallas kernels: 0 us -> 478 us
  matrix products: 360 us -> 0 us
  blocking collectives: 195 us -> 0 us
  waiting for transfers between devices: 106 us -> 0 us
  local copies, waits for them, and re-layouts: 61.7 us -> 12.2 us
  other arithmetic: 43.2 us -> 8.41 us
    pallas_call x0 -> x4, Pallas kernels: none -> 478 us  [the longest x1 365 us: mlp(): pl.pallas_call(mlp_kernel, out_shape=(jax.ShapeDtypeStruct((TOK, D), BF16...]
    dot_general x11 -> x0, matrix products: 360 us -> none  [the longest x1 86.5 us: finish(): jnp.einsum('sbd,df->sbf', normed, w_up, preferred_element_type=jnp.float32)]
    all_to_all x1 -> x0, blocking collectives: 195 us -> none  [local_run(): k_local = lax.all_to_all(k_heads, 'x', 0, 2, tiled=True)]
    all_to_all x1 -> x0, waiting for transfers between devices: 106 us -> none  [local_run(): v_local = lax.all_to_all(v_heads, 'x', 0, 2, tiled=True)]
    unnamed x40 -> x17, local copies, waits for them, and re-layouts: 35.4 us -> 10.4 us
    all_to_all x2 -> x0, local copies, waits for them, and re-layouts: 23.2 us -> none  [the longest x1 15.2 us: local_run(): v_local = lax.all_to_all(v_heads, 'x', 0, 2, tiled=True)]
    select_n x1 -> x0, other arithmetic: 22.9 us -> none  [write_slots(): cache_arr = jnp.where(slot_hit, fresh_rows[step_idx][:, None], cache_arr)]
    reduce_sum x2 -> x0, other arithmetic: 9.55 us -> none  [attend(): weight_sum = jnp.sum(old_weights, axis=-1) + jnp.sum(new_weights, axis=-1)]
  transfers between devices with their start and end apart: 1 -> 0, of which waited for: 1 -> 0; matrix products, arithmetic and copies ran while one was open for 10% -> 0% of each run, Pallas kernels for 0% -> 0%
where the time goes in v1:
time: 501 us; the launch traced here: 500 us
  Pallas kernels  478 us (95%)
  local copies, waits for them, and re-layouts  12.2 us (2%)
  other arithmetic  8.41 us (2%)
    pallas_call x1, Pallas kernels, mlp(): pl.pallas_call(mlp_kernel, out_shape=(jax.ShapeDtypeStruct((TOK, D), BF16...  365 us
    pallas_call x1, Pallas kernels, attention(): pl.pallas_call(attn_kernel, grid=(4 * PER,), out_shape=(jax.ShapeDtypeStr...  48.9 us
    pallas_call x1, Pallas kernels, qkv(): pl.pallas_call(qkv_kernel, out_shape=(jax.ShapeDtypeStruct((STEPS, GROUP,...  43.8 us
    pallas_call x1, Pallas kernels, place(): pl.pallas_call(place_kernel, out_shape=(out, out), in_specs=[pl.BlockSpec...  20.4 us
    unnamed x17, local copies, waits for them, and re-layouts  10.4 us

profile of v1, /device:TPU:0, one launch (start us, length us, event | category | flops | bytes accessed | tf_op | source)
XLA Modules:
  0.0 499.7 jit_solution(8198905114276705453)
XLA Ops:
  0.6 0.0 copy-start.6
  0.6 0.8 dynamic_slice.3.pos
  1.5 1.2 bitcast_convert_fusion
  2.7 0.7 add.42
  3.4 1.7 multiply_reduce_fusion
  5.1 0.1 rsqrt.12
  5.2 0.1 add.46
  5.3 0.1 add_convert_fusion
  5.3 0.7 convert_element_type.24
  6.1 1.3 broadcast_in_dim.28
  7.4 1.0 fusion
  8.4 1.0 pad_maximum_fusion
  9.4 0.0 copy-done.6
  9.4 1.5 multiply_convert_fusion.hn
  10.8 0.0 copy-start.5
  10.8 43.8 %qkv.1 = (bf16[4,128,16,128]{3,2,1,0:T(8,128)(2,1)}, bf16[128,8,128]{2,1,0:T(8,128)(2,1)}, bf16[128,8,128]{2,1,0:T(8,128)(2,1)}) custom-call(bf16[128,5120]{1,0:T(8,128)(2,1)} %multiply_convert_fusion.hn, f32[16,32,128]{2,1,0:T(8,128)} %get-tuple-element.28.cos, f32[16,32,128]{2,1,0:T(8,128)} %get-tuple-element.29.sin, f32[1,128]{1,0:T(1,128)} %get-tuple-element.31.qg, ...), custom_call_target="tpu_custom_call" | custom-call | flops 13421772800 | bytes 31457280 | tf_op jit(solution)/shard_map/qkv/pallas_call | solution.py:146
  54.7 0.0 copy-done.5
  54.7 0.0 copy-start.2
  54.7 1.6 copy-done.2
  56.3 0.0 copy-start.3
  56.3 0.9 copy-done.3
  57.2 0.0 copy-start.4
  57.2 0.9 copy-done.4
  58.2 48.9 %attention.1 = (bf16[16,128,512]{2,1,0:T(8,128)(2,1)S(1)}, bf16[32,4,4,2,128]{4,3,2,1,0:T(2,128)(2,1)S(1)}, bf16[32,4,4,2,128]{4,3,2,1,0:T(2,128)(2,1)S(1)}) custom-call(s32[128]{0:T(128)S(1)} %copy-done.5, bf16[4,128,16,128]{3,2,1,0:T(8,128)(2,1)S(1)} %copy-done.2, bf16[128,512,128]{2,1,0:T(8,128)(2,1)} %bitcast.19, bf16[128,512,128]{2,1,0:T(8,128)(2,1)} %bitcast.20, ...), custom_call_target="tpu_custom_call" | custom-call | flops 2147483648 | bytes 37748736 | tf_op jit(solution)/shard_map/attention/pallas_call | solution.py:256
  107.1 0.0 copy-start.1
  107.1 1.3 copy-done.1
  108.4 365.3 %mlp.1 = (bf16[128,5120]{1,0:T(8,128)(2,1)}, bf16[3,32,256,2,128]{4,3,2,1,0:T(2,128)(2,1)}, bf16[3,32,256,2,128]{4,3,2,1,0:T(2,128)(2,1)}) custom-call(bf16[16,128,512]{2,1,0:T(8,128)(2,1)} %copy-done.1, bf16[128,5120]{1,0:T(8,128)(2,1)} %bitcast.21, f32[1,5120]{1,0:T(1,128)} %bitcast.23, bf16[8192,5120]{1,0:T(8,128)(2,1)} %wo.1, bf16[5120,25600]{1,0:T(8,128)(2,1)} %wg.1, ...), custom_call_target="tpu_custom_call" | custom-call | flops 111400714240 | bytes 943718400 | tf_op jit(solution)/shard_map/mlp/pallas_call | solution.py:391
  473.7 0.0 copy-start
  473.7 4.6 copy-done
  478.3 0.0 copy-start.7
  478.3 20.4 %place.1 = (bf16[32,256,4,2,128]{4,3,2,1,0:T(2,128)(2,1)}, bf16[32,256,4,2,128]{4,3,2,1,0:T(2,128)(2,1)}) custom-call(s32[32]{0:T(128)S(1)} %dynamic_slice.3.pos, bf16[128,256,2,128]{3,2,1,0:T(2,128)(2,1)} %kc.3, bf16[128,256,2,128]{3,2,1,0:T(2,128)(2,1)} %vc.3, bf16[3,32,256,2,128]{4,3,2,1,0:T(2,128)(2,1)S(1)} %copy-done, ...), custom_call_target="tpu_custom_call" | custom-call | flops 1048576 | bytes 71303168 | tf_op jit(solution)/shard_map/place/pallas_call | solution.py:471
  498.6 0.0 copy-done.7
  498.6 1.1 copy.19
  (4 shorter events, 0.0 us)
Async XLA Ops:
  0.6 8.7 %copy-start.6 = (bf16[4,32,5120]{2,1,0:T(8,128)(2,1)S(1)}, bf16[4,32,5120]{2,1,0:T(8,128)(2,1)}, u32[]{:S(2)}) copy-start(bf16[4,32,5120]{2,1,0:T(8,128)(2,1)} %param.16) | copy-start | bytes 3932164
  10.8 43.8 %copy-start.5 = (s32[128]{0:T(128)S(1)}, s32[128]{0:T(128)}, u32[]{:S(2)}) copy-start(s32[128]{0:T(128)} %pos.1) | copy-start | bytes 1540
  54.7 1.6 copy-start.2
  56.3 0.9 copy-start.3
  57.2 0.9 copy-start.4
  107.1 1.3 copy-start.1
  473.7 4.6 copy-start
  478.3 20.4 %copy-start.7 = (bf16[128,5120]{1,0:T(8,128)(2,1)S(1)}, bf16[128,5120]{1,0:T(8,128)(2,1)}, u32[]{:S(2)}) copy-start(bf16[128,5120]{1,0:T(8,128)(2,1)} %get-tuple-element.18) | copy-start | bytes 3932164

commit v2 on v0

v2 whole, which is shorter than its diff:
```python
import jax
import jax.numpy as jnp
from jax import lax
from jax.experimental import pallas as pl
from jax.experimental.pallas import tpu as pltpu
from jax.sharding import PartitionSpec as P

EPS = 1e-6
THETA = 1000000.0
F32 = jnp.float32
BF16 = jnp.bfloat16
MESH = pl.DeviceIdType.MESH

STEPS = 4
ROWS = 32
TOK = STEPS * ROWS
GROUP = 128
D = 5120
HD = 128
QH = 16
FF = 25600
T = 256
SEQ = 4
PER = ROWS // SEQ
NS = 2
NR = 4
NC = 5
N_O = 32
N_C = FF // 256
N_D = FF // 256
PARTS = ((0, 2), (2, 1), (3, 1), (4, 1), (5, 27))


def partners(me):
    c1 = me + 1 - 2 * lax.rem(me, 2)
    c2 = lax.rem(me + 2, 4)
    c3 = 3 - me
    return c1, c2, c3


def greet(devices):
    barrier = pltpu.get_barrier_semaphore()
    for dev in devices:
        pl.semaphore_signal(barrier, inc=1, device_id={"x": dev}, device_id_type=MESH)
    pl.semaphore_wait(barrier, len(devices))


def remote(src, dst, ssem, rsem, dev):
    return pltpu.make_async_remote_copy(
        src_ref=src, dst_ref=dst, send_sem=ssem, recv_sem=rsem,
        device_id={"x": dev}, device_id_type=MESH)


def block_copies(kc, vc, k_rx, v_rx, sems, me, first, count, at):
    ks, kr, vs, vr = sems
    copies = []
    for k, dev in ((1, (me + 2) % 4), (2, 3 - me), (0, partners(me)[0])):
        rows = pl.ds(dev * ROWS + first, count)
        for src, dst, ss, rs in ((kc, k_rx, ks, kr), (vc, v_rx, vs, vr)):
            copies.append(remote(src.at[rows], dst.at[k, pl.ds(at, count)], ss.at[k], rs.at[k], dev))
    return copies


def layer_kernel(pos, gain, gain2, cos, sin, qg, kg, hid, wq, wk, wv, wo, wg, wu, wd, kc, vc, kc2, vc2,
                 out, kn_rx, vn_rx, k_rx, v_rx,
                 ws, wrow, hall, hn, tscr, kscr, vscr, q, kn, vn, kbuf, vbuf, o_rx, acc,
                 wsem, osem, s1, r1, s2, r2, sf, rf, kvsem, so, ro, sk, rk, sv, rv, lsem,
                 rsem, csem, ks, kr, vs, vr):
    me = lax.axis_index("x")
    c1, c2, c3 = partners(me)
    order = (c2, c3, c1, me)

    def bulk(part):
        first, count = PARTS[part]
        return block_copies(kc, vc, k_rx, v_rx, [sem.at[part] for sem in (ks, kr, vs, vr)], me, first, count, first)

    def start_bulk(part):
        for cp in bulk(part):
            cp.start()

    def row_o(i):
        slot = lax.rem(i, NR)
        return pltpu.make_async_copy(wo.at[pl.ds(i * 256, 256)], wrow.at[slot], rsem.at[slot])

    def row_d(i):
        slot = lax.rem(i + N_O, NR)
        return pltpu.make_async_copy(wd.at[pl.ds(i * 256, 256)], wrow.at[slot], rsem.at[slot])

    def col(i):
        slot = lax.rem(i, NC)
        at = pl.ds(pl.multiple_of(i * 256, 256), 256)
        return (pltpu.make_async_copy(wg.at[:, at], ws.at[2 * slot], csem.at[slot, 0]),
                pltpu.make_async_copy(wu.at[:, at], ws.at[2 * slot + 1], csem.at[slot, 1]))

    def owner(step):
        which = step // PER
        return jnp.where(which == 0, c2, jnp.where(which == 1, c3, jnp.where(which == 2, c1, me)))

    def base_of(step):
        return owner(step) * ROWS + lax.rem(step, PER) * SEQ

    def kv_loads(step):
        slot = lax.rem(step, NS)
        rows = pl.ds(base_of(step), SEQ)
        return (pltpu.make_async_copy(kc2.at[rows], kbuf.at[slot], kvsem.at[slot, 0]),
                pltpu.make_async_copy(vc2.at[rows], vbuf.at[slot], kvsem.at[slot, 1]))

    wcopies = []
    for c in range(10):
        if c < 8:
            src = wq.at[:, pl.ds(pl.multiple_of(me * 2048 + c * 256, 256), 256)]
        else:
            src = (wk if c == 8 else wv).at[:, pl.ds(pl.multiple_of(me * 256, 256), 256)]
        wcopies.append(pltpu.make_async_copy(src, ws.at[c], wsem.at[c]))

    greet((c1, c2, c3))
    cross = []
    fwd = []
    for s in range(STEPS):
        row = 256 + (s // 2) * 128 + (s % 2) * 32
        cross.append(remote(hid.at[pl.ds(s * 32, 32)], hall.at[pl.ds(row, 32)], s2.at[s], r2.at[s], c2))
        fwd.append(remote(hall.at[pl.ds(row, 32)], hall.at[pl.ds(row + 64, 32)], sf.at[s], rf.at[s], c1))
    for cp in cross:
        cp.start()
    near = remote(hid, hall.at[pl.ds(128, 128)], s1, r1, c1)
    near.start()
    own = pltpu.make_async_copy(hid, hall.at[pl.ds(0, 128)], osem)
    own.start()
    for cp in wcopies:
        cp.start()
    start_bulk(0)
    for step in range(NS):
        for cp in kv_loads(step):
            cp.start()
    for i in range(NR):
        row_o(i).start()

    def table(ref, groups):
        return jnp.concatenate([ref[j * STEPS + s] for j, s in groups], axis=0)

    for blk in range(4):
        if blk == 0:
            own.wait()
            groups = [(me, s) for s in range(4)]
        elif blk == 1:
            near.wait_recv()
            groups = [(c1, s) for s in range(4)]
        else:
            lo = (blk - 2) * 2
            for s in (lo, lo + 1):
                cross[s].wait_recv()
                fwd[s].start()
            for s in (lo, lo + 1):
                fwd[s].wait_recv()
            groups = [(c2, lo), (c2, lo + 1), (c3, lo), (c3, lo + 1)]

        def norm_step(r, carry, blk=blk):
            val = hall[pl.ds(blk * 128 + r * 16, 16), :].astype(F32)
            inv = lax.rsqrt(jnp.mean(val * val, axis=-1, keepdims=True) + EPS)
            hn[pl.ds(r * 16, 16), :] = (val * inv * gain[...]).astype(BF16)
            return carry

        lax.fori_loop(0, 8, norm_step, 0)
        cos_b = table(cos, groups)
        sin_b = table(sin, groups)

        def head(val, head_gain, cos_b=cos_b, sin_b=sin_b):
            inv = lax.rsqrt(jnp.mean(val * val, axis=-1, keepdims=True) + EPS)
            val = val * inv * head_gain
            return val * cos_b + pltpu.roll(val, 64, 1) * sin_b

        def project(c):
            return jnp.dot(hn[...], ws[c], preferred_element_type=F32)

        def q_chunk(c, carry, head=head):
            val = project(c)
            for hh in range(2):
                tscr[pl.ds(2 * c + hh, 128, stride=QH), :] = head(val[:, hh * HD:(hh + 1) * HD], qg[...])
            return carry

        if blk == 0:
            for cp in wcopies:
                cp.wait()
        lax.fori_loop(0, 8, q_chunk, 0)
        k_acc = project(8)
        v_acc = project(9)
        for hh in range(2):
            k_head = head(k_acc[:, hh * HD:(hh + 1) * HD], kg[...])
            v_head = v_acc[:, hh * HD:(hh + 1) * HD]
            for g, (j, s) in enumerate(groups):
                at = pl.ds(j * 256 + s * 2 + hh, 32, stride=8)
                kscr[at, :] = k_head[g * 32:(g + 1) * 32]
                vscr[at, :] = v_head[g * 32:(g + 1) * 32]
        for g, (j, s) in enumerate(groups):
            q[s, pl.ds(j * 32, 32)] = tscr[pl.ds(g * 512, 512), :].reshape(32, QH, HD).astype(BF16)
    kn[...] = kscr[...].reshape(GROUP, 8, HD).astype(BF16)
    vn[...] = vscr[...].reshape(GROUP, 8, HD).astype(BF16)
    for s in range(STEPS):
        cross[s].wait_send()
        fwd[s].wait_send()
    near.wait_send()

    def o_copy(k):
        return remote(hall.at[pl.ds(k * TOK, TOK), pl.ds(0, 2048)],
                      o_rx.at[:, pl.ds(pl.multiple_of(me * 2048, 2048), 2048)], so.at[k], ro.at[k], order[k])

    def n_copies(k):
        rows = pl.ds(order[k] * ROWS, ROWS)
        return (remote(kn.at[rows], kn_rx.at[me], sk.at[k], rk.at[k], order[k]),
                remote(vn.at[rows], vn_rx.at[me], sv.at[k], rv.at[k], order[k]))

    own_rows = pl.ds(me * ROWS, ROWS)
    own_new = (pltpu.make_async_copy(kn.at[own_rows], kn_rx.at[me], lsem.at[0]),
               pltpu.make_async_copy(vn.at[own_rows], vn_rx.at[me], lsem.at[1]))

    row = lax.broadcasted_iota(jnp.int32, (64, 2 * T), 0)
    lane = lax.broadcasted_iota(jnp.int32, (64, 2 * T), 1)
    same_head = lax.rem(row // 8, 2) == lax.rem(lane, 2)
    nrow = lax.broadcasted_iota(jnp.int32, (64, 8), 0)
    nlane = lax.broadcasted_iota(jnp.int32, (64, 8), 1)
    new_ok = (lax.rem(nrow // 8, 2) == lax.rem(nlane, 2)) & (nlane // 2 <= nrow // 16)
    scale = HD ** -0.5
    dims = (((1,), (1,)), ((), ()))

    for k in range(4):
        def attend(j, carry, k=k):
            step = k * PER + j
            slot = lax.rem(step, NS)
            base = base_of(step)
            for cp in kv_loads(step):
                cp.wait()
            for i in range(SEQ):
                start = pos[base + i]
                q2 = q[:, base + i].reshape(64, HD)
                s_old = lax.dot_general(q2, kbuf[slot, i], dims, preferred_element_type=F32) * scale
                s_old = jnp.where(same_head & (lane < 2 * start), s_old, -jnp.inf)
                s_new = lax.dot_general(q2, kn[base + i], dims, preferred_element_type=F32) * scale
                s_new = jnp.where(new_ok, s_new, -jnp.inf)
                peak = jnp.maximum(jnp.max(s_old, axis=-1, keepdims=True), jnp.max(s_new, axis=-1, keepdims=True))
                w_old = jnp.exp(s_old - peak)
                w_new = jnp.exp(s_new - peak)
                total = jnp.sum(w_old, axis=-1, keepdims=True) + jnp.sum(w_new, axis=-1, keepdims=True)
                mixed = jnp.dot(w_old.astype(BF16), vbuf[slot, i], preferred_element_type=F32)
                mixed = mixed + jnp.dot(w_new.astype(BF16), vn[base + i], preferred_element_type=F32)
                tscr[pl.ds(j * SEQ + i, 64, stride=ROWS), :] = mixed / total

            @pl.when(step + NS < 4 * PER)
            def _():
                for cp in kv_loads(step + NS):
                    cp.start()

            @pl.when(j == 1)
            def _():
                if k == 0:
                    for kk in range(3):
                        for cp in n_copies(kk):
                            cp.start()
                    for cp in own_new:
                        cp.start()
                    start_bulk(1)
                else:
                    o_copy(k - 1).start()
                    start_bulk(k + 1)
            return carry

        if k == 0:
            for i in range(NC):
                for cp in col(i):
                    cp.start()
        lax.fori_loop(0, PER, attend, 0)
        for s in range(STEPS):
            for hg in range(QH):
                val = tscr[pl.ds((s * QH + hg) * ROWS, ROWS), :].astype(BF16)
                if k < 3:
                    hall[k * TOK + s * ROWS:k * TOK + (s + 1) * ROWS, hg * HD:(hg + 1) * HD] = val
                else:
                    o_rx[s * ROWS:(s + 1) * ROWS, pl.ds(pl.multiple_of(me * 2048 + hg * HD, HD), HD)] = val

    acc[...] = jnp.zeros_like(acc)
    for k in (2, 0, 1):
        o_copy(k).wait()

    def accumulate(lhs, slot):
        for n in range(10):
            cols = slice(n * 512, (n + 1) * 512)
            acc[:, cols] = acc[:, cols] + jnp.dot(lhs, wrow[slot, :, cols], preferred_element_type=F32)

    def o_step(i, carry):
        row_o(i).wait()
        accumulate(o_rx[:, pl.ds(pl.multiple_of(i * 256, 256), 256)], lax.rem(i, NR))

        @pl.when(i + NR < N_O)
        def _():
            row_o(i + NR).start()

        @pl.when(i + NR >= N_O)
        def _():
            row_d(i + NR - N_O).start()
        return carry

    lax.fori_loop(0, N_O, o_step, 0)

    def norm2_step(r, carry):
        rows = pl.ds(r * 16, 16)
        res = (hid[rows, :].astype(F32) + acc[rows, :]).astype(BF16)
        out[rows, :] = res
        res = res.astype(F32)
        inv = lax.rsqrt(jnp.mean(res * res, axis=-1, keepdims=True) + EPS)
        hn[rows, :] = (res * inv * gain2[...]).astype(BF16)
        acc[rows, :] = jnp.zeros((16, D), F32)
        return carry

    lax.fori_loop(0, TOK // 16, norm2_step, 0)

    def act_at(i):
        return pl.ds((i // 20) * 128, 128), pl.ds(pl.multiple_of(lax.rem(i, 20) * 256, 256), 256)

    def col_step(i, carry):
        slot = lax.rem(i, NC)
        for cp in col(i):
            cp.wait()
        gate = jnp.dot(hn[...], ws[2 * slot], preferred_element_type=F32)
        up = jnp.dot(hn[...], ws[2 * slot + 1], preferred_element_type=F32)
        rows, cols = act_at(i)
        hall[rows, cols] = (gate * jax.nn.sigmoid(gate) * up).astype(BF16)

        @pl.when(i + NC < N_C)
        def _():
            for cp in col(i + NC):
                cp.start()
        return carry

    lax.fori_loop(0, N_C, col_step, 0)

    def d_step(i, carry):
        row_d(i).wait()
        rows, cols = act_at(i)
        accumulate(hall[rows, cols], lax.rem(i + N_O, NR))

        @pl.when(i + NR < N_D)
        def _():
            row_d(i + NR).start()
        return carry

    lax.fori_loop(0, N_D, d_step, 0)

    def out_step(r, carry):
        rows = pl.ds(r * 16, 16)
        out[rows, :] = (out[rows, :].astype(F32) + acc[rows, :]).astype(BF16)
        return carry

    lax.fori_loop(0, TOK // 16, out_step, 0)
    for k in range(3):
        for cp in n_copies(k):
            cp.wait()
    for cp in own_new:
        cp.wait()
    for part in range(len(PARTS)):
        for cp in bulk(part):
            cp.wait()


def layer(pos, gain, gain2, cos, sin, qg, kg, hid, wq, wk, wv, wo, wg, wu, wd, kc, vc):
    vmem = pl.BlockSpec(memory_space=pltpu.VMEM)
    hbm = pl.BlockSpec(memory_space=pl.ANY)
    dma = pltpu.SemaphoreType.DMA
    new = jax.ShapeDtypeStruct((4, ROWS, 8, HD), BF16)
    rx = jax.ShapeDtypeStruct((3, ROWS, T, 2, HD), BF16)
    n_parts = len(PARTS)
    return pl.pallas_call(
        layer_kernel,
        out_shape=(jax.ShapeDtypeStruct((TOK, D), BF16), new, new, rx, rx),
        in_specs=[pl.BlockSpec(memory_space=pltpu.SMEM)] + [vmem] * 7 + [hbm] * 11,
        out_specs=(vmem,) + (hbm,) * 4,
        scratch_shapes=[
            pltpu.VMEM((10, D, 256), BF16),
            pltpu.VMEM((NR, 256, D), BF16),
            pltpu.VMEM((640, D), BF16),
            pltpu.VMEM((TOK, D), BF16),
            pltpu.VMEM((2048, HD), F32),
            pltpu.VMEM((GROUP * 8, HD), F32), pltpu.VMEM((GROUP * 8, HD), F32),
            pltpu.VMEM((STEPS, GROUP, QH, HD), BF16),
            pltpu.VMEM((GROUP, 8, HD), BF16), pltpu.VMEM((GROUP, 8, HD), BF16),
            pltpu.VMEM((NS, SEQ, 2 * T, HD), BF16), pltpu.VMEM((NS, SEQ, 2 * T, HD), BF16),
            pltpu.VMEM((TOK, 8192), BF16),
            pltpu.VMEM((TOK, D), F32),
            dma((10,)), dma, dma, dma, dma((4,)), dma((4,)), dma((4,)), dma((4,)), dma((NS, 2)),
            dma((3,)), dma((3,)), dma((3,)), dma((3,)), dma((3,)), dma((3,)), dma((2,)),
            dma((NR,)), dma((NC, 2)),
            dma((n_parts, 3)), dma((n_parts, 3)), dma((n_parts, 3)), dma((n_parts, 3))],
        compiler_params=pltpu.CompilerParams(collective_id=0, has_side_effects=True, vmem_limit_bytes=67043328),
        cost_estimate=pl.CostEstimate(flops=2 * TOK * D * (18432 + 3 * FF), bytes_accessed=1000 << 20, transcendentals=0),
        name="layer",
    )(pos, gain, gain2, cos, sin, qg, kg, hid, wq, wk, wv, wo, wg, wu, wd, kc, vc,
      kc.reshape(GROUP, 2 * T, HD), vc.reshape(GROUP, 2 * T, HD))


AR = 8


def place_kernel(pos, kc, vc, k_rx, v_rx, kn, vn, k_out, v_out, kbuf, vbuf, isem, osem):
    me = lax.axis_index("x")
    c1, c2, c3 = partners(me)
    arrays = ((kc, k_rx, kn, k_out, kbuf), (vc, v_rx, vn, v_out, vbuf))

    def loads(i):
        slot = i % AR
        copies = []
        for a, (own, rx, _, _, buf) in enumerate(arrays):
            for k, dev in enumerate((c1, c2, c3)):
                copies.append(pltpu.make_async_copy(
                    rx.at[k, i], buf.at[slot, :, dev], isem.at[slot, a, k]))
            copies.append(pltpu.make_async_copy(
                own.at[me * ROWS + i], buf.at[slot, :, me], isem.at[slot, a, 3]))
        return copies

    def stores(i):
        slot = i % AR
        return [pltpu.make_async_copy(buf.at[slot], out.at[i], osem.at[slot, a])
                for a, (_, _, _, out, buf) in enumerate(arrays)]

    incoming = {}
    outgoing = {}
    for i in range(AR - 2):
        incoming[i] = loads(i)
        for cp in incoming[i]:
            cp.start()
    for i in range(ROWS):
        for cp in incoming[i]:
            cp.wait()
        start = pos[i]
        for _, _, new, _, buf in arrays:
            for s in range(STEPS):
                for x in range(4):
                    buf[i % AR, start + s, x] = new[x, i, s]
        outgoing[i] = stores(i)
        for cp in outgoing[i]:
            cp.start()
        if i >= 2:
            for cp in outgoing[i - 2]:
                cp.wait()
        nxt = i + AR - 2
        if nxt < ROWS:
            incoming[nxt] = loads(nxt)
            for cp in incoming[nxt]:
                cp.start()
    for i in (ROWS - 2, ROWS - 1):
        for cp in outgoing[i]:
            cp.wait()


def place(pos, kc, vc, k_rx, v_rx, kn, vn):
    hbm = pl.BlockSpec(memory_space=pl.ANY)
    vmem = pl.BlockSpec(memory_space=pltpu.VMEM)
    out = jax.ShapeDtypeStruct((ROWS, T, 4, 2, HD), BF16)
    buf = pltpu.VMEM((AR, T, 4, 2, HD), BF16)
    dma = pltpu.SemaphoreType.DMA
    return pl.pallas_call(
        place_kernel,
        out_shape=(out, out),
        in_specs=[pl.BlockSpec(memory_space=pltpu.SMEM)] + [hbm] * 4 + [vmem] * 2,
        out_specs=(hbm, hbm),
        scratch_shapes=[buf, buf, dma((AR, 2, 4)), dma((AR, 2))],
        compiler_params=pltpu.CompilerParams(vmem_limit_bytes=60 << 20),
        cost_estimate=pl.CostEstimate(flops=1 << 20, bytes_accessed=68 << 20, transcendentals=0),
        name="place",
    )(pos, kc, vc, k_rx, v_rx, kn.reshape(4, ROWS, STEPS, 2, HD), vn.reshape(4, ROWS, STEPS, 2, HD))


def solution(mesh):
    row_spec = P(None, ('dp', 'x'), None)
    cache_in = P('dp', None, 'x', None)
    cache_out = P(('dp', 'x'), None, None, None)

    def local_run(start_pos, hidden_in, k_heads, v_heads, attn_norm, w_q, w_k, w_v, q_norm, k_norm, w_o, mlp_norm, w_gate, w_up, w_down):
        my_pos = lax.dynamic_slice_in_dim(start_pos, lax.axis_index('x') * ROWS, ROWS)
        hid = hidden_in.reshape(TOK, D)

        half = jnp.power(THETA, -jnp.arange(HD // 2, dtype=F32) * 2.0 / HD)
        inv_freq = jnp.concatenate([half, half])
        sign = jnp.where(jnp.arange(HD) < HD // 2, -1.0, 1.0).astype(F32)
        positions = start_pos.reshape(4, 1, ROWS) + jnp.arange(STEPS)[None, :, None]
        angles = positions.astype(F32)[..., None] * inv_freq
        cos = jnp.cos(angles).reshape(16, ROWS, HD)
        sin = (jnp.sin(angles) * sign).reshape(16, ROWS, HD)

        out, kn, vn, k_rx, v_rx = layer(
            start_pos, attn_norm.astype(F32)[None], mlp_norm.astype(F32)[None], cos, sin,
            q_norm.astype(F32)[None], k_norm.astype(F32)[None], hid,
            w_q, w_k, w_v, w_o, w_gate, w_up, w_down, k_heads, v_heads)
        k_out, v_out = place(my_pos, k_heads, v_heads, k_rx, v_rx, kn, vn)
        return (out.reshape(STEPS, ROWS, D), k_out.reshape(ROWS, T, 8, HD), v_out.reshape(ROWS, T, 8, HD))

    return jax.shard_map(local_run, mesh=mesh, in_specs=(P('dp'), row_spec, cache_in, cache_in) + (P(),) * 11, out_specs=(row_spec, cache_out, cache_out), check_vma=False)
```

time: 784 us -> 459 us (0.59); the launches traced: 775 us -> 458 us
  Pallas kernels: 0 us -> 449 us
  matrix products: 360 us -> 0 us
  blocking collectives: 195 us -> 0 us
  waiting for transfers between devices: 106 us -> 0 us
  local copies, waits for them, and re-layouts: 61.7 us -> 3.13 us
  other arithmetic: 43.2 us -> 5.84 us
    pallas_call x0 -> x2, Pallas kernels: none -> 449 us  [the longest x1 424 us: layer(): pl.pallas_call(layer_kernel, out_shape=(jax.ShapeDtypeStruct((TOK, D), BF...]
    dot_general x11 -> x0, matrix products: 360 us -> none  [the longest x1 86.5 us: finish(): jnp.einsum('sbd,df->sbf', normed, w_up, preferred_element_type=jnp.float32)]
    all_to_all x1 -> x0, blocking collectives: 195 us -> none  [local_run(): k_local = lax.all_to_all(k_heads, 'x', 0, 2, tiled=True)]
    all_to_all x1 -> x0, waiting for transfers between devices: 106 us -> none  [local_run(): v_local = lax.all_to_all(v_heads, 'x', 0, 2, tiled=True)]
    unnamed x40 -> x3, local copies, waits for them, and re-layouts: 35.4 us -> 1.06 us
    all_to_all x2 -> x0, local copies, waits for them, and re-layouts: 23.2 us -> none  [the longest x1 15.2 us: local_run(): v_local = lax.all_to_all(v_heads, 'x', 0, 2, tiled=True)]
    select_n x1, other arithmetic: 22.9 us -> 0.08 us  [local_run(): sign = jnp.where(jnp.arange(HD) < HD // 2, -1.0, 1.0).astype(F32)]
    reduce_sum x5 -> x0, other arithmetic: 11.3 us -> none  [the longest x2 9.55 us: attend(): weight_sum = jnp.sum(old_weights, axis=-1) + jnp.sum(new_weights, axis=-1)]
  transfers between devices with their start and end apart: 1 -> 0, of which waited for: 1 -> 0; matrix products, arithmetic and copies ran while one was open for 10% -> 0% of each run, Pallas kernels for 0% -> 0%
where the time goes in v2:
time: 459 us; the launch traced here: 458 us
  Pallas kernels  449 us (98%)
  other arithmetic  5.84 us (1%)
    pallas_call x1, Pallas kernels, layer(): pl.pallas_call(layer_kernel, out_shape=(jax.ShapeDtypeStruct((TOK, D), BF...  424 us
    pallas_call x1, Pallas kernels, place(): pl.pallas_call(place_kernel, out_shape=(out, out), in_specs=[pl.BlockSpec...  24.7 us

profile of v2, /device:TPU:0, one launch (start us, length us, event | category | flops | bytes accessed | tf_op | source)
XLA Modules:
  0.0 458.4 jit_solution(12811033503024997596)
XLA Ops:
  0.6 1.2 dynamic_slice.3.pos
  1.9 0.1 compare_select_fusion
  2.0 1.3 bitcast_convert_fusion
  3.2 0.7 add.28
  4.0 0.1 add.32
  4.1 0.1 add_convert_fusion
  4.1 1.3 broadcast_in_dim.42
  5.5 1.3 broadcast_in_dim.43
  6.8 1.8 fusion
  8.5 424.1 %layer.1 = (bf16[128,5120]{1,0:T(8,128)(2,1)}, bf16[4,32,8,128]{3,2,1,0:T(8,128)(2,1)}, bf16[4,32,8,128]{3,2,1,0:T(8,128)(2,1)}, bf16[3,32,256,2,128]{4,3,2,1,0:T(2,128)(2,1)}, bf16[3,32,256,2,128]{4,3,2,1,0:T(2,128)(2,1)}) custom-call(s32[128]{0:T(128)} %pos.1, f32[1,5120]{1,0:T(1,128)} %bitcast.23, f32[1,5120]{1,0:T(1,128)} %bitcast.24, ...), custom_call_target="tpu_custom_call" | custom-call | flops 124822487040 | bytes 1048576000 | tf_op jit(solution)/shard_map/layer/pallas_call | solution.py:370
  432.6 0.0 copy-start
  432.6 24.7 %place.1 = (bf16[32,256,4,2,128]{4,3,2,1,0:T(2,128)(2,1)}, bf16[32,256,4,2,128]{4,3,2,1,0:T(2,128)(2,1)}) custom-call(s32[32]{0:T(128)} %dynamic_slice.3.pos, bf16[128,256,2,128]{3,2,1,0:T(2,128)(2,1)} %kc.3, bf16[128,256,2,128]{3,2,1,0:T(2,128)(2,1)} %vc.3, bf16[3,32,256,2,128]{4,3,2,1,0:T(2,128)(2,1)} %get-tuple-element.11.k_rx, ...), custom_call_target="tpu_custom_call" | custom-call | flops 1048576 | bytes 71303168 | tf_op jit(solution)/shard_map/place/pallas_call | solution.py:458
  457.4 0.0 copy-done
  457.4 1.1 copy.19
  (3 shorter events, 0.0 us)
Async XLA Ops:
  432.6 24.7 %copy-start = (bf16[128,5120]{1,0:T(8,128)(2,1)S(1)}, bf16[128,5120]{1,0:T(8,128)(2,1)}, u32[]{:S(2)}) copy-start(bf16[128,5120]{1,0:T(8,128)(2,1)} %get-tuple-element.10) | copy-start | bytes 3932164
